TPU v7x, 32 devices: a whole 2x2x4 slice. The times are simulated.
32 devices in a mesh: rows: 8 (over y, x, core), cols: 4 (over z).
Axes of the slice: x: 2, y: 2, z: 4, core: 2. Of those that a mesh axis runs over, the one named last changes fastest.
Arguments:
- token_ids: int32 [16, 2048], P('rows', 'cols'), may hold values from 0 to 131071, as said below
- lengths: int32 [16], P('rows'), may hold values from 1 to 2048
- table: bfloat16 [131072, 512], P('rows', 'cols'), may hold values from -6 to 6
- attn_gain: float32 [512], replicated, may hold values from 0.1 to 1.9
- w_qkv: bfloat16 [512, 1536], replicated, may hold values from -2 to 2
- w_out: bfloat16 [512, 512], replicated, may hold values from -0.25 to 0.25
- mlp_gain: float32 [512], replicated, may hold values from 0.1 to 1.9
- w_in: bfloat16 [512, 4096], replicated, may hold values from -0.25 to 0.25
- w_down: bfloat16 [2048, 512], replicated, may hold values from -0.125 to 0.125
Outputs:
- layer_out: bfloat16 [16, 2048, 512], P('rows', 'cols')
Inputs may be any that keep to these rules, and one draw needn't show every extreme that they name: `token_ids`: ids lie in 0 to 131071. In each aligned block of 2 histories (4096 positions) at most 1365 ids fall in any one block of 16384 consecutive table rows, and in every such block of histories some block of table rows receives exactly 1365.
All inputs are finite; a program needn't handle non-finite values.
Results may differ from a plain program's by a relative error of at most 0.012.
Values may be sent and summed in bfloat16 or wider, within the bound.
A program may use at most 192 MiB of HBM per device.

v0:
```python
import jax
import jax.numpy as jnp
from jax import lax
from jax.sharding import PartitionSpec as P

D = 512
HEADS = 8
FF = 2048


def rms_norm(values_f32, gain):
    mean_sq = jnp.mean(values_f32 * values_f32, axis=-1, keepdims=True)
    return values_f32 * lax.rsqrt(mean_sq + 1e-06) * gain


def local(token_ids, lengths, table, attn_gain, w_qkv, w_out, mlp_gain, w_in, w_down):
    batch_dev, quarter = token_ids.shape
    col_count = lax.axis_size("cols")
    row_count = lax.axis_size("rows")
    full_len = quarter * col_count
    block_rows, col_width = table.shape
    zero_bf = jnp.zeros((), jnp.bfloat16)
    own_ids = lax.all_gather(token_ids, "cols", axis=1, tiled=True)
    flat_ids = own_ids.reshape(-1)
    token_count = flat_ids.shape[0]
    capacity = 8 * token_count // (3 * row_count)
    owner_block = flat_ids // block_rows
    onehot = (owner_block[:, None] == jnp.arange(row_count, dtype=jnp.int32)[None, :]).astype(
        jnp.int32
    )
    slot_rank = jnp.sum((jnp.cumsum(onehot, axis=0) - 1) * onehot, axis=1)
    slot_index = owner_block * capacity + slot_rank
    requests = jnp.full((row_count * capacity,), -1, jnp.int32)
    requests = (
        requests.at[slot_index]
        .set(flat_ids - owner_block * block_rows)
        .reshape(row_count, capacity)
    )
    asked = lax.all_to_all(requests, "rows", split_axis=0, concat_axis=0, tiled=True)
    looked = jnp.take(table, jnp.maximum(asked, 0), axis=0)
    looked = jnp.where((asked >= 0)[..., None], looked, zero_bf)
    returned = lax.all_to_all(looked, "rows", split_axis=0, concat_axis=0, tiled=True)
    embedded = returned.reshape(row_count * capacity, col_width)[slot_index]
    embedded = embedded.reshape(batch_dev, full_len, col_width)
    sequence = lax.all_to_all(embedded, "cols", split_axis=1, concat_axis=2, tiled=True)
    residual = sequence.astype(jnp.float32)
    normed = rms_norm(residual, attn_gain).astype(jnp.bfloat16)
    projected = jnp.einsum("bqe,ef->bqf", normed, w_qkv, preferred_element_type=jnp.float32).astype(
        jnp.bfloat16
    )
    head_dim = D // HEADS
    queries = projected[..., :D].reshape(batch_dev, quarter, HEADS, head_dim)
    keys = projected[..., D : 2 * D]
    values = projected[..., 2 * D :]
    query_pos = lax.axis_index("cols") * quarter + jnp.arange(quarter, dtype=jnp.int32)
    running_max = jnp.full((batch_dev, HEADS, quarter), -1e30, jnp.float32)
    key_piece = lax.all_gather(keys, "cols", axis=1, tiled=True)
    value_piece = lax.all_gather(values, "cols", axis=1, tiled=True)
    piece_len = key_piece.shape[1]
    key_heads = key_piece.reshape(batch_dev, piece_len, HEADS, head_dim)
    value_heads = value_piece.reshape(batch_dev, piece_len, HEADS, head_dim)
    scores = (
        jnp.einsum("bqhd,bkhd->bhqk", queries, key_heads, preferred_element_type=jnp.float32)
        * 0.125
    )
    key_pos = jnp.arange(piece_len, dtype=jnp.int32)
    causal = key_pos[None, :] <= query_pos[:, None]
    inside = key_pos[None, :] < lengths[:, None]
    valid = causal[None, None, :, :] & inside[:, None, None, :]
    scores = jnp.where(valid, scores, -1e30)
    new_max = jnp.maximum(running_max, jnp.max(scores, axis=-1))
    probs = jnp.where(valid, jnp.exp(scores - new_max[..., None]), 0.0)
    running_sum = jnp.sum(probs, axis=-1)
    weighted = jnp.einsum(
        "bhqk,bkhd->bhqd",
        probs.astype(jnp.bfloat16),
        value_heads,
        preferred_element_type=jnp.float32,
    )
    final_max, final_sum, weighted = (new_max, running_sum, weighted)
    summed = weighted / final_sum[..., None]
    attended = (
        jnp.transpose(summed, (0, 2, 1, 3)).reshape(batch_dev, quarter, D).astype(jnp.bfloat16)
    )
    hidden = (
        residual + jnp.einsum("bqe,ef->bqf", attended, w_out, preferred_element_type=jnp.float32)
    ).astype(jnp.bfloat16)
    hidden_f32 = hidden.astype(jnp.float32)
    normed_two = rms_norm(hidden_f32, mlp_gain).astype(jnp.bfloat16)
    gate_up = jnp.einsum("bqe,ef->bqf", normed_two, w_in, preferred_element_type=jnp.float32)
    act = (jax.nn.silu(gate_up[..., :FF]) * gate_up[..., FF:]).astype(jnp.bfloat16)
    return (
        hidden_f32 + jnp.einsum("bqf,fe->bqe", act, w_down, preferred_element_type=jnp.float32)
    ).astype(jnp.bfloat16)


def solution(mesh):
    in_specs = (P("rows", "cols"), P("rows"), P("rows", "cols"), P(), P(), P(), P(), P(), P())
    out_specs = P("rows", "cols", None)
    return jax.shard_map(local, mesh=mesh, in_specs=in_specs, out_specs=out_specs, check_vma=False)
```

profile of v0, /device:TPU:0, one launch (start us, length us, event | category | flops | bytes accessed | tf_op | source)
XLA Modules:
  0.0 414.5 jit_solution(13161058633130101524)
XLA Ops:
  6.5 0.0 copy-start
  6.5 15.2 %all_gather.9 = s32[2,2048]{1,0:T(2,128)S(1)} all-gather(s32[2,512]{1,0:T(2,128)} %param.9), channel_id=1, replica_groups=mesh['rows'=8,'cols'=4] {'cols'}, dimensions={1}, use_global_device_ids=true | all-gather | bytes 20480 | tf_op jit(solution)/shard_map/all_gather | solution.py:23
  21.8 2.3 reduce-window.6
  24.1 0.3 slice_reduce_fusion
  24.4 0.2 reduce-window.9
  24.6 0.1 add_bitcast_fusion
  24.8 0.1 fusion.32
  24.9 0.1 compare_select_fusion
  25.0 15.5 %scatter_custom_fusion = s32[10920]{0:T(1024)S(1)} fusion(s32[4096]{0:T(1024)S(1)} %bitcast.81, s32[4096]{0:T(1024)S(1)} %get-tuple-element.10, s32[]{:T(128)} %constant.27.clone.1), kind=kCustom, calls=%fused_computation.65 | custom fusion | bytes 43684 | tf_op jit(solution)/shard_map/scatter | solution.py:36
  40.5 0.1 all_to_all.16
  40.6 8.4 %all_to_all.23 = s32[8,1,1365]{2,1,0:T(1,128)S(1)} all-to-all(s32[8,1,1365]{2,1,0:T(1,128)S(1)} %all_to_all.16), channel_id=1, replica_groups=mesh['rows'=8,'cols'=4] {'rows'}, dimensions={0} | all-to-all | bytes 87360 | tf_op jit(solution)/shard_map/all_to_all | solution.py:39
  49.1 0.1 reshape.265
  49.2 23.7 %gather_fusion = bf16[10920,128]{1,0:T(8,128)(2,1)} fusion(bf16[16384,128]{1,0:T(8,128)(2,1)} %param.11, s32[11264]{0:T(1024)S(1)} %pad_clamp_fusion), kind=kCustom, calls=%fused_computation | custom fusion | bytes 5634720 | tf_op jit(solution)/shard_map/jit(_take)/gather | solution.py:40
  72.9 4.2 %reshape.264 = bf16[8,1365,128]{2,1,0:T(8,128)(2,1)} reshape(bf16[10920,128]{1,0:T(8,128)(2,1)} %gather_fusion) | data formatting | bytes 5591040 | tf_op jit(solution)/shard_map/jit(_take)/gather | solution.py:40
  77.1 10.2 %select_select_fusion = bf16[8,1365,128]{2,1,0:T(8,128)(2,1)} fusion(bf16[8,1365,128]{2,1,0:T(8,128)(2,1)} %reshape.264, pred[8,1365]{1,0:T(8,128)(4,1)S(1)} %get-tuple-element.9, pred[8,1365]{1,0:T(8,128)(4,1)S(1)} %get-tuple-element.8), kind=kLoop, calls=%fused_computation.21 | loop fusion | flops 2795520 | bytes 5612880 | tf_op jit(solution)/shard_map/jit(_where)/select_n | solution.py:41
  87.3 4.4 %all-to-all-start.1 = ((bf16[8,1365,128]{2,1,0:T(8,128)(2,1)}), bf16[8,1365,128]{2,1,0:T(8,128)(2,1)}, u32[]{:S(2)}, u32[]{:S(2)}) async-start(bf16[8,1365,128]{2,1,0:T(8,128)(2,1)} %select_select_fusion), calls=%async_computation.1 | async-start | bytes 5603328 | tf_op jit(solution)/shard_map/all_to_all | solution.py:42
  91.7 0.0 all-gather.3.cloned.1.call-start
  91.8 34.1 %all-to-all-done.1 = bf16[8,1365,128]{2,1,0:T(8,128)(2,1)} async-done(((bf16[8,1365,128]{2,1,0:T(8,128)(2,1)}), bf16[8,1365,128]{2,1,0:T(8,128)(2,1)}, u32[]{:S(2)}, u32[]{:S(2)}) %all-to-all-start.1) | async-done | bytes 2795552 | tf_op jit(solution)/shard_map/all_to_all | solution.py:42
  125.9 4.2 %reshape.256 = bf16[10920,128]{1,0:T(8,128)(2,1)} reshape(bf16[8,1365,128]{2,1,0:T(8,128)(2,1)} %all-to-all-done.1) | data formatting | bytes 5591040 | tf_op jit(solution)/shard_map/reshape | solution.py:43
  130.1 13.2 %gather_fusion.1 = bf16[4096,128]{1,0:T(8,128)(2,1)S(1)} fusion(bf16[10920,128]{1,0:T(8,128)(2,1)} %reshape.256, s32[4096]{0:T(1024)S(1)} %broadcast_clamp_fusion), kind=kCustom, calls=%fused_computation.1 | custom fusion | bytes 2113536 | tf_op jit(solution)/shard_map/gather | solution.py:43
  143.3 8.7 %copy.57 = bf16[2,2048,128]{2,0,1:T(2,128)(2,1)S(1)} copy(bf16[2,2048,128]{2,1,0:T(8,128)(2,1)S(1)} %bitcast.75) | data formatting | bytes 2097152 | tf_op jit(solution)/shard_map/reshape | solution.py:44
  152.0 27.2 %all_to_all.24 = bf16[2,2048,128]{2,0,1:T(2,128)(2,1)S(1)} all-to-all(bf16[2,2048,128]{2,0,1:T(2,128)(2,1)S(1)} %copy.57), channel_id=1, replica_groups=mesh['rows'=8,'cols'=4] {'cols'}, dimensions={1} | all-to-all | bytes 2097152 | tf_op jit(solution)/shard_map/all_to_all | solution.py:45
  179.2 0.0 copy-start.2
  179.2 1.5 copy_convert_fusion
  180.7 2.9 copy.59
  183.6 0.6 multiply_reduce_fusion
  184.3 0.0 copy-done.2
  184.3 1.8 fusion.18
  186.2 3.2 convolution_convert_fusion
  189.4 0.0 copy-start.3
  189.4 1.7 fusion.44
  191.1 0.0 all-gather.3.cloned.1.call-update
  191.1 0.0 all-gather.5.cloned.1.call-start
  191.2 0.0 copy-done.3
  191.2 0.1 iota_compare_fusion.3
  191.3 0.7 iota_compare_fusion
  191.9 2.6 broadcast_and_fusion
  194.6 1.3 copy.61
  195.9 0.0 all-gather.5.cloned.1.call-update
  195.9 76.4 %all-gather.3.cloned.1.call-done = bf16[2,2048,512]{2,1,0:T(8,128)(2,1)} async-done(((bf16[2,512,512]{2,1,0:T(8,128)(2,1)}), bf16[2,2048,512]{2,1,0:T(8,128)(2,1)}) %all-gather.3.cloned.1.call-update) | async-done | bytes 4194320 | tf_op jit(solution)/shard_map/all_gather | solution.py:57
  272.4 6.3 %copy.62 = bf16[2,2048,512]{1,2,0:T(8,128)(2,1)} copy(bf16[2,2048,512]{2,1,0:T(8,128)(2,1)} %all-gather.3.cloned.1.call-done) | data formatting | bytes 8388608 | tf_op jit(solution)/shard_map/all_gather | solution.py:57
  278.6 0.0 copy-start.1
  278.6 27.7 %fusion = (f32[2,8,512]{2,1,0:T(8,128)S(1)}, f32[2,8,512,2048]{3,2,1,0:T(8,128)}) fusion(pred[2,512,2048]{2,1,0:T(8,128)(4,1)} %broadcast_and_fusion, bf16[2,512,8,64]{1,3,2,0:T(8,128)(2,1)} %bitcast.74, bf16[2,2048,8,64]{1,3,2,0:T(8,128)(2,1)} %bitcast.72), kind=kOutput, calls=%fused_computation.5 | convolution fusion | flops 2197807104 | bytes 74481664 | tf_op jit(solution)/shard_map/bqhd,bkhd->bhqk/dot_general | solution.py:63
  306.3 0.0 copy-done.1
  306.3 22.4 %fusion.1 = f32[2,8,512]{2,1,0:T(8,128)S(1)} fusion(f32[2,8,512,2048]{3,2,1,0:T(8,128)} %get-tuple-element.13, f32[2,8,512]{2,1,0:T(8,128)S(1)} %broadcast_maximum_fusion, pred[2,512,2048]{2,1,0:T(8,128)(4,1)S(1)} %copy-done.1), kind=kLoop, calls=%fused_computation.6 | loop fusion | flops 83877888 | bytes 69271552 | tf_op jit(solution)/shard_map/reduce_sum | solution.py:73
  328.7 24.5 %all-gather.5.cloned.1.call-done = bf16[2,2048,512]{2,1,0:T(8,128)(2,1)} async-done(((bf16[2,512,512]{2,1,0:T(8,128)(2,1)}), bf16[2,2048,512]{2,1,0:T(8,128)(2,1)}) %all-gather.5.cloned.1.call-update) | async-done | bytes 4194320 | tf_op jit(solution)/shard_map/all_gather | solution.py:58
  353.2 6.3 %copy.63 = bf16[2,2048,512]{1,2,0:T(8,128)(2,1)} copy(bf16[2,2048,512]{2,1,0:T(8,128)(2,1)} %all-gather.5.cloned.1.call-done) | data formatting | bytes 8388608 | tf_op jit(solution)/shard_map/all_gather | solution.py:58
  359.5 27.0 %fusion.16 = bf16[2,512,8,64]{1,3,2,0:T(8,128)(2,1)S(1)} fusion(bf16[2,2048,8,64]{1,3,2,0:T(8,128)(2,1)} %bitcast.76, f32[2,8,512,2048]{3,2,1,0:T(8,128)} %get-tuple-element.13, f32[2,8,512]{2,1,0:T(8,128)S(1)} %broadcast_maximum_fusion, pred[2,512,2048]{2,1,0:T(8,128)(4,1)} %broadcast_and_fusion, f32[2,512,8]{1,2,0:T(8,128)S(1)} %bitcast.85), kind=kOutput, calls=%fused_computation.28 | convolution fusion | flops 2232418304 | bytes 74514432 | tf_op jit(solution)/shard_map/bhqk,bkhd->bhqd/dot_general | solution.py:74
  386.5 0.0 copy-start.4
  386.5 0.0 copy-start.5
  386.5 2.7 fusion.11
  389.2 0.3 copy-done.4
  389.4 0.0 copy-done.5
  389.4 8.3 %fusion.7 = f32[2,512,4096]{2,1,0:T(8,128)} fusion(bf16[512,4096]{1,0:T(8,128)(2,1)S(1)} %copy-done.4, bf16[2,512,512]{1,2,0:T(8,128)(2,1)S(1)} %get-tuple-element.15, f32[512]{0:T(512)S(1)} %copy-done.5, f32[2,512]{1,0:T(2,128)S(1)} %add_rsqrt_fusion), kind=kOutput, calls=%fused_computation.12 | convolution fusion | flops 4297064448 | bytes 22026240 | tf_op jit(solution)/shard_map/bqe,ef->bqf/dot_general | solution.py:90
  397.8 0.0 copy-done
  397.8 8.6 %fusion.14 = bf16[2,512,512]{1,2,0:T(8,128)(2,1)S(1)} fusion(bf16[2,512,512]{1,2,0:T(8,128)(2,1)S(1)} %get-tuple-element.15, bf16[2048,512]{1,0:T(8,128)(2,1)S(1)} %copy-done, f32[2,512,4096]{2,1,0:T(8,128)} %fusion.7), kind=kOutput, calls=%fused_computation.25 | convolution fusion | flops 2161639424 | bytes 20971520 | tf_op jit(solution)/shard_map/bqf,fe->bqe/dot_general | solution.py:93
  406.3 1.3 copy.68
  (16 shorter events, 0.2 us)
Async XLA Ops:
  6.5 391.2 %copy-start = (bf16[2048,512]{1,0:T(8,128)(2,1)S(1)}, bf16[2048,512]{1,0:T(8,128)(2,1)}, u32[]{:S(2)}) copy-start(bf16[2048,512]{1,0:T(8,128)(2,1)} %param.17) | copy-start | bytes 6291460
  87.3 38.6 %all-to-all-start.1 = ((bf16[8,1365,128]{2,1,0:T(8,128)(2,1)}), bf16[8,1365,128]{2,1,0:T(8,128)(2,1)}, u32[]{:S(2)}, u32[]{:S(2)}) async-start(bf16[8,1365,128]{2,1,0:T(8,128)(2,1)} %select_select_fusion), calls=%async_computation.1 | async-start | bytes 5603328 | tf_op jit(solution)/shard_map/all_to_all | solution.py:42
  91.7 180.7 %all-gather.3.cloned.1.call-start = ((), (), s32[]{:S(2)}) async-start(), calls=%async_computation.3 | async-start | bytes 5242880 | tf_op jit(solution)/shard_map/all_gather | solution.py:57
  179.2 5.1 %copy-start.2 = (f32[512]{0:T(512)S(1)}, f32[512]{0:T(512)}, u32[]{:S(2)}) copy-start(f32[512]{0:T(512)} %param.12) | copy-start | bytes 6148
  189.4 1.8 copy-start.3
  191.1 162.1 %all-gather.5.cloned.1.call-start = ((), (), s32[]{:S(2)}) async-start(), calls=%async_computation.4 | async-start | bytes 5242880 | tf_op jit(solution)/shard_map/all_gather | solution.py:58
  278.6 27.7 %copy-start.1 = (pred[2,512,2048]{2,1,0:T(8,128)(4,1)S(1)}, pred[2,512,2048]{2,1,0:T(8,128)(4,1)}, u32[]{:S(2)}) copy-start(pred[2,512,2048]{2,1,0:T(8,128)(4,1)} %broadcast_and_fusion) | copy-start | bytes 6291460
  386.5 3.0 copy-start.4
  386.5 3.0 copy-start.5
Sparse Core Ops, SparseCore 0:
  191.2 81.0 all-gather.2
  273.9 79.2 all-gather.4
where the time goes:
time: 415 us
  waiting for transfers between devices  135 us (33%)
  local copies, waits for them, and re-layouts  90.2 us (22%)
  matrix products  77.4 us (19%)
  blocking collectives  50.8 us (12%)
  other arithmetic  42.8 us (10%)
  between operations  13.7 us (3%)
  starting transfers between devices  4.49 us (1%)
    all_gather x1, waiting for transfers between devices, local(): key_piece = lax.all_gather(keys, 'cols', axis=1, tiled=True)  76.4 us
    all_to_all x1, waiting for transfers between devices, local(): lax.all_to_all(looked, 'rows', split_axis=0, concat_axis=0, tiled=True)  34.1 us
    gather x2, local copies, waits for them, and re-layouts, local(): looked = jnp.take(table, jnp.maximum(asked, 0), axis=0)  27.9 us
    dot_general x1, matrix products, local(): jnp.einsum('bqhd,bkhd->bhqk', queries, key_heads, preferred_element_type=...  27.7 us
    all_to_all x1, blocking collectives, local(): lax.all_to_all(embedded, 'cols', split_axis=1, concat_axis=2, tiled=True)  27.2 us
    dot_general x1, matrix products, local(): jnp.einsum('bhqk,bkhd->bhqd', probs.astype(jnp.bfloat16), value_heads, pr...  27 us
    all_gather x1, waiting for transfers between devices, local(): value_piece = lax.all_gather(values, 'cols', axis=1, tiled=True)  24.5 us
    reduce_sum x1, other arithmetic, local(): running_sum = jnp.sum(probs, axis=-1)  22.4 us
  transfers between devices with their start and end apart: 3, of which 3 were waited for; matrix products, arithmetic and copies ran while one was open for 15% of the time, Pallas kernels for 0%

commit v1 on v0

--- a/solution.py
+++ b/solution.py
@@ -54,8 +54,11 @@
     values = projected[..., 2 * D :]
     query_pos = lax.axis_index("cols") * quarter + jnp.arange(quarter, dtype=jnp.int32)
     running_max = jnp.full((batch_dev, HEADS, quarter), -1e30, jnp.float32)
-    key_piece = lax.all_gather(keys, "cols", axis=1, tiled=True)
-    value_piece = lax.all_gather(values, "cols", axis=1, tiled=True)
+    key_piece, value_piece = jnp.split(
+        lax.all_gather(jnp.concatenate([keys, values], axis=0), "cols", axis=1, tiled=True),
+        [keys.shape[0]],
+        axis=0,
+    )
     piece_len = key_piece.shape[1]
     key_heads = key_piece.reshape(batch_dev, piece_len, HEADS, head_dim)
     value_heads = value_piece.reshape(batch_dev, piece_len, HEADS, head_dim)

time: 415 us -> 465 us (1.12)
  waiting for transfers between devices: 135 us -> 180 us
    all_gather x2 -> x1, waiting for transfers between devices: 101 us -> 145 us  [local(): lax.all_gather(jnp.concatenate([keys, values], axis=0), 'cols', axis=1, t...]
    split x0 -> x3, local copies, waits for them, and re-layouts: none -> 18.4 us  [local(): jnp.split(lax.all_gather(jnp.concatenate([keys, values], axis=0), 'cols',...]
    all_gather x2 -> x0, local copies, waits for them, and re-layouts: 12.6 us -> none  [the longest x1 6.28 us: local(): key_piece = lax.all_gather(keys, 'cols', axis=1, tiled=True)]
  transfers between devices with their start and end apart: 3 -> 2, of which waited for: 3 -> 2; matrix products, arithmetic and copies ran while one was open for 15% -> 1% of each run, Pallas kernels for 0% -> 0%
where the time goes in v1:
time: 465 us; the launch traced here: 464 us
  waiting for transfers between devices  180 us (39%)
  local copies, waits for them, and re-layouts  94.6 us (20%)
  matrix products  77 us (17%)
  blocking collectives  50.8 us (11%)
  other arithmetic  44.4 us (10%)
  between operations  13.7 us (3%)
    all_gather x1, waiting for transfers between devices, local(): lax.all_gather(jnp.concatenate([keys, values], axis=0), 'cols', axis=1, t...  145 us
    all_to_all x1, waiting for transfers between devices, local(): lax.all_to_all(looked, 'rows', split_axis=0, concat_axis=0, tiled=True)  34.1 us
    gather x2, local copies, waits for them, and re-layouts, local(): looked = jnp.take(table, jnp.maximum(asked, 0), axis=0)  27.9 us
    all_to_all x1, blocking collectives, local(): lax.all_to_all(embedded, 'cols', split_axis=1, concat_axis=2, tiled=True)  27.2 us
    dot_general x1, matrix products, local(): jnp.einsum('bhqk,bkhd->bhqd', probs.astype(jnp.bfloat16), value_heads, pr...  27.1 us
    dot_general x1, matrix products, local(): jnp.einsum('bqhd,bkhd->bhqk', queries, key_heads, preferred_element_type=...  27.1 us
    reduce_sum x1, other arithmetic, local(): running_sum = jnp.sum(probs, axis=-1)  22.4 us
    split x3, local copies, waits for them, and re-layouts, local(): jnp.split(lax.all_gather(jnp.concatenate([keys, values], axis=0), 'cols',...  18.4 us
  transfers between devices with their start and end apart: 2, of which 2 were waited for; matrix products, arithmetic and copies ran while one was open for 1% of the time, Pallas kernels for 0%

profile of v1, /device:TPU:0, one launch (start us, length us, event | category | flops | bytes accessed | tf_op | source)
XLA Modules:
  0.0 464.4 jit_solution(17055649674703634112)
XLA Ops:
  6.5 0.0 copy-start
  6.5 15.2 %all_gather.6 = s32[2,2048]{1,0:T(2,128)S(1)} all-gather(s32[2,512]{1,0:T(2,128)} %param.9), channel_id=1, replica_groups=mesh['rows'=8,'cols'=4] {'cols'}, dimensions={1}, use_global_device_ids=true | all-gather | bytes 20480 | tf_op jit(solution)/shard_map/all_gather | solution.py:23
  21.8 2.3 reduce-window.6
  24.1 0.3 slice_reduce_fusion
  24.5 0.2 reduce-window.9
  24.6 0.1 add_bitcast_fusion
  24.8 0.1 fusion.32
  24.9 0.1 compare_select_fusion
  25.0 15.5 %scatter_custom_fusion = s32[10920]{0:T(1024)S(1)} fusion(s32[4096]{0:T(1024)S(1)} %bitcast.82, s32[4096]{0:T(1024)S(1)} %get-tuple-element.12, s32[]{:T(128)} %constant.27.clone.1), kind=kCustom, calls=%fused_computation.66 | custom fusion | bytes 43684 | tf_op jit(solution)/shard_map/scatter | solution.py:36
  40.5 0.1 all_to_all.16
  40.6 8.4 %all_to_all.23 = s32[8,1,1365]{2,1,0:T(1,128)S(1)} all-to-all(s32[8,1,1365]{2,1,0:T(1,128)S(1)} %all_to_all.16), channel_id=1, replica_groups=mesh['rows'=8,'cols'=4] {'rows'}, dimensions={0} | all-to-all | bytes 87360 | tf_op jit(solution)/shard_map/all_to_all | solution.py:39
  49.1 0.1 reshape.265
  49.2 23.7 %gather_fusion = bf16[10920,128]{1,0:T(8,128)(2,1)} fusion(bf16[16384,128]{1,0:T(8,128)(2,1)} %param.11, s32[11264]{0:T(1024)S(1)} %pad_clamp_fusion), kind=kCustom, calls=%fused_computation | custom fusion | bytes 5634720 | tf_op jit(solution)/shard_map/jit(_take)/gather | solution.py:40
  72.9 4.2 reshape.264
  77.1 10.2 %select_select_fusion = bf16[8,1365,128]{2,1,0:T(8,128)(2,1)} fusion(bf16[8,1365,128]{2,1,0:T(8,128)(2,1)} %reshape.264, pred[8,1365]{1,0:T(8,128)(4,1)S(1)} %get-tuple-element.11, pred[8,1365]{1,0:T(8,128)(4,1)S(1)} %get-tuple-element.10), kind=kLoop, calls=%fused_computation.21 | loop fusion | flops 2795520 | bytes 5612880 | tf_op jit(solution)/shard_map/jit(_where)/select_n | solution.py:41
  87.3 4.4 all-to-all-start.1
  91.7 0.0 all-gather.2.cloned.1.call-start
  91.8 34.1 %all-to-all-done.1 = bf16[8,1365,128]{2,1,0:T(8,128)(2,1)} async-done(((bf16[8,1365,128]{2,1,0:T(8,128)(2,1)}), bf16[8,1365,128]{2,1,0:T(8,128)(2,1)}, u32[]{:S(2)}, u32[]{:S(2)}) %all-to-all-start.1) | async-done | bytes 2795552 | tf_op jit(solution)/shard_map/all_to_all | solution.py:42
  125.9 4.2 reshape.256
  130.1 13.2 %gather_fusion.1 = bf16[4096,128]{1,0:T(8,128)(2,1)S(1)} fusion(bf16[10920,128]{1,0:T(8,128)(2,1)} %reshape.256, s32[4096]{0:T(1024)S(1)} %broadcast_clamp_fusion), kind=kCustom, calls=%fused_computation.1 | custom fusion | bytes 2113536 | tf_op jit(solution)/shard_map/gather | solution.py:43
  143.3 8.7 %copy.57 = bf16[2,2048,128]{2,0,1:T(2,128)(2,1)S(1)} copy(bf16[2,2048,128]{2,1,0:T(8,128)(2,1)S(1)} %bitcast.76) | data formatting | bytes 2097152 | tf_op jit(solution)/shard_map/reshape | solution.py:44
  152.0 27.2 %all_to_all.24 = bf16[2,2048,128]{2,0,1:T(2,128)(2,1)S(1)} all-to-all(bf16[2,2048,128]{2,0,1:T(2,128)(2,1)S(1)} %copy.57), channel_id=1, replica_groups=mesh['rows'=8,'cols'=4] {'cols'}, dimensions={1} | all-to-all | bytes 2097152 | tf_op jit(solution)/shard_map/all_to_all | solution.py:45
  179.2 0.0 copy-start.2
  179.2 0.6 multiply_reduce_fusion
  179.9 1.5 copy_convert_fusion
  181.4 2.9 copy.59
  184.3 0.0 copy-done.2
  184.3 1.8 fusion.18
  186.2 3.2 convolution_convert_fusion
  189.4 0.2 fusion.45
  189.6 0.0 copy-start.3
  189.7 1.6 pad_maximum_fusion
  191.2 0.0 all-gather.2.cloned.1.call-update
  191.3 0.0 copy-done.3
  191.3 0.1 iota_compare_fusion.3
  191.4 0.7 iota_compare_fusion
  192.0 2.6 broadcast_and_fusion
  194.7 1.3 copy.61
  196.0 145.4 %all-gather.2.cloned.1.call-done = bf16[4,2048,512]{2,1,0:T(8,128)(2,1)} async-done(((bf16[4,512,512]{2,1,0:T(8,128)(2,1)}), bf16[4,2048,512]{2,1,0:T(8,128)(2,1)}) %all-gather.2.cloned.1.call-update) | async-done | bytes 8388624 | tf_op jit(solution)/shard_map/all_gather | solution.py:58
  341.4 5.7 %fusion.44 = (bf16[2,2048,512]{2,1,0:T(8,128)(2,1)}, bf16[2,2048,512]{2,1,0:T(8,128)(2,1)}) fusion(bf16[4,2048,512]{2,1,0:T(8,128)(2,1)} %all-gather.2.cloned.1.call-done), kind=kLoop, calls=%fused_computation.85 | loop fusion | bytes 16777216 | tf_op jit(solution)/shard_map/split | solution.py:57
  347.1 6.3 %copy.62 = bf16[2,2048,512]{1,2,0:T(8,128)(2,1)} copy(bf16[2,2048,512]{2,1,0:T(8,128)(2,1)} %get-tuple-element.5) | data formatting | bytes 8388608 | tf_op jit(solution)/shard_map/split | solution.py:57
  353.4 6.4 %copy.63 = bf16[2,2048,512]{1,2,0:T(8,128)(2,1)} copy(bf16[2,2048,512]{2,1,0:T(8,128)(2,1)} %get-tuple-element.6) | data formatting | bytes 8388608 | tf_op jit(solution)/shard_map/split | solution.py:57
  359.8 0.0 copy-start.1
  359.8 27.1 %fusion = (f32[2,8,512]{2,1,0:T(8,128)S(1)}, f32[2,8,512,2048]{3,2,1,0:T(8,128)}) fusion(pred[2,512,2048]{2,1,0:T(8,128)(4,1)} %broadcast_and_fusion, bf16[2,512,8,64]{1,3,2,0:T(8,128)(2,1)} %bitcast.75, bf16[2,2048,8,64]{1,3,2,0:T(8,128)(2,1)} %bitcast.73), kind=kOutput, calls=%fused_computation.5 | convolution fusion | flops 2197807104 | bytes 74481664 | tf_op jit(solution)/shard_map/bqhd,bkhd->bhqk/dot_general | solution.py:66
  386.9 0.0 copy-done.1
  386.9 22.4 %fusion.1 = f32[2,8,512]{2,1,0:T(8,128)S(1)} fusion(f32[2,8,512,2048]{3,2,1,0:T(8,128)} %get-tuple-element.15, f32[2,8,512]{2,1,0:T(8,128)S(1)} %broadcast_maximum_fusion, pred[2,512,2048]{2,1,0:T(8,128)(4,1)S(1)} %copy-done.1), kind=kLoop, calls=%fused_computation.6 | loop fusion | flops 83877888 | bytes 69271552 | tf_op jit(solution)/shard_map/reduce_sum | solution.py:76
  409.2 27.1 %fusion.16 = bf16[2,512,8,64]{1,3,2,0:T(8,128)(2,1)S(1)} fusion(bf16[2,2048,8,64]{1,3,2,0:T(8,128)(2,1)} %bitcast.77, f32[2,8,512,2048]{3,2,1,0:T(8,128)} %get-tuple-element.15, f32[2,8,512]{2,1,0:T(8,128)S(1)} %broadcast_maximum_fusion, pred[2,512,2048]{2,1,0:T(8,128)(4,1)} %broadcast_and_fusion, f32[2,512,8]{1,2,0:T(8,128)S(1)} %bitcast.86), kind=kOutput, calls=%fused_computation.29 | convolution fusion | flops 2232418304 | bytes 74514432 | tf_op jit(solution)/shard_map/bhqk,bkhd->bhqd/dot_general | solution.py:77
  436.4 0.0 copy-start.4
  436.4 0.0 copy-start.5
  436.4 2.7 fusion.11
  439.1 0.3 copy-done.4
  439.4 0.0 copy-done.5
  439.4 8.3 %fusion.7 = f32[2,512,4096]{2,1,0:T(8,128)} fusion(bf16[512,4096]{1,0:T(8,128)(2,1)S(1)} %copy-done.4, bf16[2,512,512]{1,2,0:T(8,128)(2,1)S(1)} %get-tuple-element.17, f32[512]{0:T(512)S(1)} %copy-done.5, f32[2,512]{1,0:T(2,128)S(1)} %add_rsqrt_fusion), kind=kOutput, calls=%fused_computation.12 | convolution fusion | flops 4297064448 | bytes 22026240 | tf_op jit(solution)/shard_map/bqe,ef->bqf/dot_general | solution.py:93
  447.7 0.0 copy-done
  447.7 8.6 %fusion.14 = bf16[2,512,512]{1,2,0:T(8,128)(2,1)S(1)} fusion(bf16[2,512,512]{1,2,0:T(8,128)(2,1)S(1)} %get-tuple-element.17, bf16[2048,512]{1,0:T(8,128)(2,1)S(1)} %copy-done, f32[2,512,4096]{2,1,0:T(8,128)} %fusion.7), kind=kOutput, calls=%fused_computation.25 | convolution fusion | flops 2161639424 | bytes 20971520 | tf_op jit(solution)/shard_map/bqf,fe->bqe/dot_general | solution.py:96
  456.3 1.3 copy.68
  (16 shorter events, 0.2 us)
Async XLA Ops:
  6.5 441.2 %copy-start = (bf16[2048,512]{1,0:T(8,128)(2,1)S(1)}, bf16[2048,512]{1,0:T(8,128)(2,1)}, u32[]{:S(2)}) copy-start(bf16[2048,512]{1,0:T(8,128)(2,1)} %param.17) | copy-start | bytes 6291460
  87.3 38.6 %all-to-all-start.1 = ((bf16[8,1365,128]{2,1,0:T(8,128)(2,1)}), bf16[8,1365,128]{2,1,0:T(8,128)(2,1)}, u32[]{:S(2)}, u32[]{:S(2)}) async-start(bf16[8,1365,128]{2,1,0:T(8,128)(2,1)} %select_select_fusion), calls=%async_computation.1 | async-start | bytes 5603328 | tf_op jit(solution)/shard_map/all_to_all | solution.py:42
  91.7 249.7 %all-gather.2.cloned.1.call-start = ((), (), s32[]{:S(2)}) async-start(), calls=%async_computation.3 | async-start | bytes 10485760 | tf_op jit(solution)/shard_map/all_gather | solution.py:58
  179.2 5.1 %copy-start.2 = (f32[512]{0:T(512)S(1)}, f32[512]{0:T(512)}, u32[]{:S(2)}) copy-start(f32[512]{0:T(512)} %param.12) | copy-start | bytes 6148
  189.6 1.6 copy-start.3
  359.8 27.1 %copy-start.1 = (pred[2,512,2048]{2,1,0:T(8,128)(4,1)S(1)}, pred[2,512,2048]{2,1,0:T(8,128)(4,1)}, u32[]{:S(2)}) copy-start(pred[2,512,2048]{2,1,0:T(8,128)(4,1)} %broadcast_and_fusion) | copy-start | bytes 6291460
  436.4 3.0 copy-start.4
  436.4 3.0 copy-start.5
Sparse Core Ops, SparseCore 0:
  191.4 149.9 all-gather.1
